TPU v7x, 256 devices: a whole 4x4x8 slice. The times are simulated.
256 devices in a mesh: radial: 64 (over x, z, core), phi: 4 (over y).
Axes of the slice: x: 4, y: 4, z: 8, core: 2. Of those that a mesh axis runs over, the one named last changes fastest.
Arguments:
- conserved: float32 [8, 512, 64, 128], P(None, 'radial', 'phi'), may hold values from -2.5 to 7, as said below
- core_mass: float32 [1], replicated, may hold values from 0.2 to 1
Outputs:
- advanced: float32 [8, 512, 64, 128], P(None, 'radial', 'phi')
- enclosed_mass: float32 [512], P('radial')
Inputs may be any that keep to these rules, and one draw needn't show every extreme that they name: conserved[0] (density) lies between 0.4 and 2.5; conserved[4] exceeds (conserved[1]^2 + conserved[2]^2 + conserved[3]^2)/(2 conserved[0]) by at least 0.6; the speeds |conserved[m]/conserved[0]| stay below 1; conserved[5..7] lie between 0 and conserved[0].
All inputs are finite; a program needn't handle non-finite values.
Results may differ from a plain program's by a relative error of at most 0.0003.
Values sent between devices are 32-bit elements; how exact they have to be, the bound alone decides.
A program may use at most 64 MiB of HBM per device.

v0:
```python
import math

import jax
import jax.numpy as jnp
from jax import lax
from jax.sharding import PartitionSpec as P

ADIABATIC = 4.0 / 3.0
INNER_RADIUS = 1.0
OUTER_RADIUS = 2.0
COURANT = 0.4
GRAVITY_KICK = 0.004
MINIMUM_DENSITY = 0.05
PRESSURE_FLOOR = 0.01


def from_everyone(value, axis):
    peers = lax.axis_size(axis)
    return lax.all_to_all(
        jnp.broadcast_to(value[None], (peers, *value.shape)), axis, 0, 0, tiled=True
    )


def taken_together(value, axis):
    return from_everyone(value, axis).sum(axis=0)


def combined_pairwise(pieces, combine):
    while len(jax.tree.leaves(pieces)[0]) > 1:
        pieces = jax.vmap(combine)(*(pieces[side::2] for side in (0, 1)))
    return pieces[0]


def entering(value, axis, combine, identity):
    peers, place = (lax.axis_size(axis), lax.axis_index(axis))
    passed = jnp.arange(peers) < place

    def kept(part, zero, own):
        part = jnp.where(
            passed.reshape(-1, *(1 for _ in own.shape)), part, jnp.asarray(zero, own.dtype)
        )
        return part

    pieces = from_everyone(value, axis)
    return combined_pairwise(kept(pieces, identity, value), combine)


def extended_2(value, sides, width, wrap):
    for axis, dim in sides:
        peers, length = (lax.axis_size(axis), value.shape[dim])
        up = [(i, (i + 1) % peers) for i in range(peers if wrap else peers - 1)]
        down = [(j, i) for i, j in up]
        last = lax.slice_in_dim(value, length - width, length, axis=dim)
        initial = lax.slice_in_dim(value, 0, width, axis=dim)
        before = lax.ppermute(last, axis, up)
        after = lax.ppermute(initial, axis, down)
        value = jnp.concatenate([before, value, after], axis=dim)
    return value


def step_sizes(radial_total, phi_total, theta_total):
    theta_step = math.pi / theta_total
    phi_step = 2.0 * math.pi / phi_total
    polar_width = INNER_RADIUS * math.sin(0.5 * theta_step) * phi_step
    radial_step = min(2.0 * polar_width, (OUTER_RADIUS - INNER_RADIUS) / radial_total)
    timestep = COURANT * min(radial_step, polar_width)
    return (radial_step, theta_step, phi_step, timestep)


def thermo(values):
    density = jnp.maximum(values[0], MINIMUM_DENSITY)
    kinetic = (
        0.5 * (values[1] * values[1] + values[2] * values[2] + values[3] * values[3]) / density
    )
    pressure = jnp.maximum((ADIABATIC - 1.0) * (values[4] - kinetic), PRESSURE_FLOOR * density)
    return (density, pressure)


def physical(values, component):
    density, pressure = thermo(values)
    normal = values[component] / density
    sound = jnp.sqrt(ADIABATIC * pressure / density)
    pieces = [values[which] * normal for which in range(values.shape[0])]
    pieces[component] = pieces[component] + pressure
    pieces[4] = pieces[4] + pressure * normal
    return (jnp.stack(pieces), jnp.abs(normal) + sound)


def face_flux(values, along_dim, component):
    interior = values.shape[along_dim] - 4
    neighbour_differences = lax.slice_in_dim(
        values, 1, interior + 4, axis=along_dim
    ) - lax.slice_in_dim(values, 0, interior + 3, axis=along_dim)
    below_diff = lax.slice_in_dim(neighbour_differences, 0, interior + 2, axis=along_dim)
    above_diff = lax.slice_in_dim(neighbour_differences, 1, interior + 3, axis=along_dim)
    limited = (
        0.5
        * (jnp.sign(below_diff) + jnp.sign(above_diff))
        * jnp.minimum(jnp.abs(below_diff), jnp.abs(above_diff))
    )
    left_state = lax.slice_in_dim(values, 1, interior + 2, axis=along_dim) + 0.5 * lax.slice_in_dim(
        limited, 0, interior + 1, axis=along_dim
    )
    right_state = lax.slice_in_dim(
        values, 2, interior + 3, axis=along_dim
    ) - 0.5 * lax.slice_in_dim(limited, 1, interior + 2, axis=along_dim)
    left_flux, left_signal = physical(left_state, component)
    right_flux, right_signal = physical(right_state, component)
    signal = jnp.maximum(left_signal, right_signal)
    return 0.5 * (left_flux + right_flux) - 0.5 * signal * (right_state - left_state)


def hydro_rate(extended, cell_centers, enclosed, radial_step, theta_step, phi_step, strength):
    theta_cells = extended.shape[3]
    centre_cells = extended[:, 2:-2, 2:-2, :]
    polar_padded = jnp.pad(centre_cells, ((0, 0), (0, 0), (0, 0), (2, 2)), mode="edge")
    radial_flux = face_flux(extended[:, :, 2:-2, :], 1, 1)
    polar_flux = face_flux(polar_padded, 3, 2)
    azimuth_flux = face_flux(extended[:, 2:-2, :, :], 2, 3)
    angles = (jnp.arange(theta_cells, dtype=jnp.float32) + 0.5) * theta_step
    sine_center = jnp.sin(angles)
    cosine = jnp.cos(angles)
    face_sine = jnp.sin(jnp.arange(theta_cells + 1, dtype=jnp.float32) * theta_step)
    radius = cell_centers[:, None, None]
    face_radius = jnp.concatenate(
        [cell_centers - 0.5 * radial_step, cell_centers[-1:] + 0.5 * radial_step]
    )[:, None, None]
    radial_area = face_radius * face_radius * radial_flux
    divergence = (radial_area[:, 1:] - radial_area[:, :-1]) / (radius * radius * radial_step)
    polar_area = face_sine * polar_flux
    divergence = divergence + (polar_area[..., 1:] - polar_area[..., :-1]) / (
        radius * sine_center * theta_step
    )
    divergence = divergence + (azimuth_flux[:, :, 1:] - azimuth_flux[:, :, :-1]) / (
        radius * sine_center * phi_step
    )
    density, pressure = thermo(centre_cells)
    radial_speed = centre_cells[1] / density
    polar_speed = centre_cells[2] / density
    azimuth_speed = centre_cells[3] / density
    cotangent = cosine / sine_center
    gravity_pull = strength * enclosed[:, None, None] / (radius * radius)
    source_radial = (
        2.0 * pressure + density * (polar_speed * polar_speed + azimuth_speed * azimuth_speed)
    ) / radius - density * gravity_pull
    source_polar = (
        pressure * cotangent
        + density * azimuth_speed * azimuth_speed * cotangent
        - density * radial_speed * polar_speed
    ) / radius
    source_azimuth = -density * azimuth_speed * (radial_speed + polar_speed * cotangent) / radius
    source_energy = -centre_cells[1] * gravity_pull
    nothing = jnp.zeros_like(pressure)
    source = jnp.stack(
        [
            nothing,
            source_radial,
            source_polar,
            source_azimuth,
            source_energy,
            nothing,
            nothing,
            nothing,
        ]
    )
    return source - divergence


def add_terms(earlier, later):
    return earlier + later


def body(conserved, core_mass):
    radial_rows = conserved.shape[1]
    phi_cells = conserved.shape[2]
    theta_cells = conserved.shape[3]
    radial_devices = lax.axis_size("radial")
    position = lax.axis_index("radial")
    radial_step, theta_step, phi_step, timestep = step_sizes(
        radial_rows * radial_devices, phi_cells * lax.axis_size("phi"), theta_cells
    )
    strength = GRAVITY_KICK / timestep
    first_row = position * radial_rows
    cell_centers = (
        INNER_RADIUS
        + ((first_row + jnp.arange(radial_rows, dtype=jnp.int32)).astype(jnp.float32) + 0.5)
        * radial_step
    )
    sine_center = jnp.sin((jnp.arange(theta_cells, dtype=jnp.float32) + 0.5) * theta_step)
    local_shells = jnp.dot(
        jnp.sum(conserved[0], axis=1), sine_center, precision=lax.Precision.HIGHEST
    )
    local_shells = (
        local_shells * cell_centers * cell_centers * (radial_step * theta_step * phi_step)
    )
    shells = taken_together(local_shells, "phi")
    before = entering(jnp.sum(shells), "radial", add_terms, jnp.float32(0.0))
    enclosed = core_mass[0] + before + jnp.cumsum(shells) - 0.5 * shells

    def clipped_rows(extended, halo_width):
        total_rows = extended.shape[1]
        low_rows = jnp.where(
            position == 0,
            lax.slice_in_dim(extended, halo_width, halo_width + 1, axis=1),
            lax.slice_in_dim(extended, 0, halo_width, axis=1),
        )
        high_rows = jnp.where(
            position == radial_devices - 1,
            lax.slice_in_dim(
                extended, total_rows - halo_width - 1, total_rows - halo_width, axis=1
            ),
            lax.slice_in_dim(extended, total_rows - halo_width, total_rows, axis=1),
        )
        middle = lax.slice_in_dim(extended, halo_width, total_rows - halo_width, axis=1)
        return jnp.concatenate([low_rows, middle, high_rows], axis=1)

    def extend(values):
        wedge_split_state = extended_2(values, (("phi", 2),), 2, True)
        slab_split_state = extended_2(wedge_split_state, (("radial", 1),), 2, False)
        return clipped_rows(slab_split_state, 2)

    section_one = conserved + timestep * hydro_rate(
        extend(conserved), cell_centers, enclosed, radial_step, theta_step, phi_step, strength
    )
    section_two = section_one + timestep * hydro_rate(
        extend(section_one), cell_centers, enclosed, radial_step, theta_step, phi_step, strength
    )
    advanced = 0.5 * conserved + 0.5 * section_two
    return (advanced, enclosed)


def solution(mesh):
    in_specs = (P(None, "radial", "phi", None), P())
    out_specs = (P(None, "radial", "phi", None), P("radial"))
    return jax.shard_map(body, mesh=mesh, in_specs=in_specs, out_specs=out_specs, check_vma=False)
```

profile of v0, /device:TPU:2, one launch (start us, length us, event | category | flops | bytes accessed | tf_op | source)
XLA Modules:
  0.0 79.3 jit_solution(11763445968841728372)
XLA Ops:
  0.6 1.1 %fusion.54 = (f32[8,8,2,128]{3,2,1,0:T(2,128)S(1)}, f32[8,8,2,128]{3,2,1,0:T(2,128)S(1)}) fusion(f32[8,8,16,128]{3,2,1,0:T(8,128)} %param.2), kind=kLoop, calls=%fused_computation.340 | loop fusion | bytes 262144 | tf_op jit(solution)/shard_map/slice | solution.py:53
  1.8 1.7 %collective-permute-start = (f32[8,8,2,128]{3,1,2,0:T(8,128)S(1)}, f32[8,8,2,128]{3,1,2,0:T(8,128)S(1)}, u32[]{:S(2)}, u32[]{:S(2)}) collective-permute-start(f32[8,8,2,128]{3,1,2,0:T(8,128)S(1)} %copy.721), channel_id=1, source_target_pairs={{0,1},{1,2},{2,3},{3,0},{4,5},{5,6},{6,7},{7,4},{8,9},{9,10},{10,1... | collective-permute-start | bytes 196616 | tf_op jit(solution)/shard_map/ppermute | solution.py:55
  3.5 1.7 %collective-permute-start.1 = (f32[8,8,2,128]{3,1,2,0:T(8,128)S(1)}, f32[8,8,2,128]{3,1,2,0:T(8,128)S(1)}, u32[]{:S(2)}, u32[]{:S(2)}) collective-permute-start(f32[8,8,2,128]{3,1,2,0:T(8,128)S(1)} %copy.722), channel_id=1, source_target_pairs={{1,0},{2,1},{3,2},{0,3},{5,4},{6,5},{7,6},{4,7},{9,8},{10,9},{11,1... | collective-permute-start | bytes 196616 | tf_op jit(solution)/shard_map/ppermute | solution.py:56
  5.1 0.9 %slice_reduce_fusion.2 = f32[8,128]{1,0:T(8,128)S(1)} fusion(f32[8,8,16,128]{3,2,1,0:T(8,128)} %param.2), kind=kLoop, calls=%fused_computation.312 | loop fusion | flops 15360 | bytes 69632
  6.0 0.2 fusion.2
  6.1 0.6 broadcast_in_dim.45
  6.7 3.3 %all-to-all-start = ((f32[4,1,8]{2,1,0:T(1,128)}), f32[4,1,8]{2,1,0:T(1,128)S(1)}, u32[]{:S(2)}, u32[]{:S(2)}) async-start(f32[4,1,8]{2,1,0:T(1,128)} %broadcast_in_dim.45), calls=%async_computation | async-start | bytes 4096 | tf_op jit(solution)/shard_map/all_to_all | solution.py:19
  10.0 0.2 fusion.53
  10.4 0.6 slice.760
  11.0 0.4 copy.723
  11.4 0.4 copy.724
  11.9 0.2 reshape.178
  12.1 0.2 reshape.179
  12.3 0.5 pad_maximum_fusion.6
  12.8 0.3 slice_subtract_fusion.1
  13.1 0.7 minimum_multiply_fusion.1
  13.9 0.8 fusion.6
  14.6 0.2 multiply_bitcast_fusion.1
  16.1 0.5 subtract_multiply_fusion.1
  16.7 0.6 fusion.48
  17.3 1.3 %broadcast_in_dim.46 = f32[64,1,1]{2,1,0:T(1,128)} broadcast(f32[]{:T(128)} %get-tuple-element.18), dimensions={} | broadcast | bytes 260 | tf_op jit(solution)/shard_map/broadcast_in_dim | solution.py:20
  18.6 12.0 %all-to-all-start.1 = ((f32[64,1,1]{2,1,0:T(1,128)}), f32[64,1,1]{2,1,0:T(1,128)S(1)}, u32[]{:S(2)}, u32[]{:S(2)}) async-start(f32[64,1,1]{2,1,0:T(1,128)} %broadcast_in_dim.46), calls=%async_computation.1 | async-start | bytes 65536 | tf_op jit(solution)/shard_map/all_to_all | solution.py:19
  31.2 0.2 reduce-window.7
  31.4 7.7 %all-to-all-done.1 = f32[64,1,1]{2,1,0:T(1,128)S(1)} async-done(((f32[64,1,1]{2,1,0:T(1,128)}), f32[64,1,1]{2,1,0:T(1,128)S(1)}, u32[]{:S(2)}, u32[]{:S(2)}) %all-to-all-start.1) | async-done | bytes 288 | tf_op jit(solution)/shard_map/all_to_all | solution.py:19
  39.1 0.6 reduce.4
  39.8 0.1 slice.749
  40.8 0.6 fusion.55
  42.7 0.5 multiply_divide_fusion
  44.0 2.8 %collective-permute-start.3 = (f32[8,2,20,128]{3,0,2,1:T(8,128)S(1)}, f32[8,2,20,128]{3,0,2,1:T(8,128)S(1)}, u32[]{:S(2)}, u32[]{:S(2)}) collective-permute-start(f32[8,2,20,128]{3,0,2,1:T(8,128)S(1)} %copy.686), channel_id=1, source_target_pairs={{4,0},{8,4},{12,8},{16,12},{20,16},{24,20},{28,24},{32,28},{36,32}... | collective-permute-start | bytes 491528 | tf_op jit(solution)/shard_map/ppermute | solution.py:56
  46.9 2.1 %collective-permute-start.2 = (f32[8,2,20,128]{3,0,2,1:T(8,128)S(1)}, f32[8,2,20,128]{3,0,2,1:T(8,128)S(1)}, u32[]{:S(2)}, u32[]{:S(2)}) collective-permute-start(f32[8,2,20,128]{3,0,2,1:T(8,128)S(1)} %copy.682), channel_id=1, source_target_pairs={{0,4},{4,8},{8,12},{12,16},{16,20},{20,24},{24,28},{28,32},{32,36}... | collective-permute-start | bytes 491528 | tf_op jit(solution)/shard_map/ppermute | solution.py:55
  49.0 0.6 minimum_multiply_fusion.3
  49.5 0.3 fusion.10
  49.8 0.2 multiply_bitcast_fusion.3
  50.4 0.2 multiply_subtract_fusion.1
  50.7 4.9 %collective-permute-done.2 = f32[8,2,20,128]{3,0,2,1:T(8,128)S(1)} collective-permute-done((f32[8,2,20,128]{3,0,2,1:T(8,128)S(1)}, f32[8,2,20,128]{3,0,2,1:T(8,128)S(1)}, u32[]{:S(2)}, u32[]{:S(2)}) %collective-permute-start.2) | collective-permute-done | bytes 163872 | tf_op jit(solution)/shard_map/ppermute | solution.py:55
  55.6 0.2 pad_maximum_fusion
  55.9 0.3 minimum_multiply_fusion.5
  56.3 0.1 multiply_bitcast_fusion.5
  56.8 0.2 subtract_multiply_fusion.3
  57.0 0.4 fusion.28
  57.4 0.5 slice_reduce_fusion.1
  57.9 2.1 %collective-permute-start.4 = (f32[8,8,2,128]{3,1,2,0:T(8,128)S(1)}, f32[8,8,2,128]{3,1,2,0:T(8,128)S(1)}, u32[]{:S(2)}, u32[]{:S(2)}) collective-permute-start(f32[8,8,2,128]{3,1,2,0:T(8,128)S(1)} %copy.696), channel_id=1, source_target_pairs={{0,1},{1,2},{2,3},{3,0},{4,5},{5,6},{6,7},{7,4},{8,9},{9,10},{10,1... | collective-permute-start | bytes 196616 | tf_op jit(solution)/shard_map/ppermute | solution.py:55
  60.0 1.3 %collective-permute-start.5 = (f32[8,8,2,128]{3,1,2,0:T(8,128)S(1)}, f32[8,8,2,128]{3,1,2,0:T(8,128)S(1)}, u32[]{:S(2)}, u32[]{:S(2)}) collective-permute-start(f32[8,8,2,128]{3,1,2,0:T(8,128)S(1)} %copy.697), channel_id=1, source_target_pairs={{1,0},{2,1},{3,2},{0,3},{5,4},{6,5},{7,6},{4,7},{9,8},{10,9},{11,1... | collective-permute-start | bytes 196616 | tf_op jit(solution)/shard_map/ppermute | solution.py:56
  61.4 0.2 reshape.180
  61.5 0.2 reshape.181
  61.7 0.5 pad_maximum_fusion.7
  62.2 0.3 slice_subtract_fusion
  62.6 0.7 minimum_multiply_fusion
  63.3 0.7 fusion.4
  64.1 0.2 multiply_bitcast_fusion
  65.1 0.5 subtract_multiply_fusion
  66.1 1.9 %collective-permute-start.6 = (f32[8,2,20,128]{3,0,2,1:T(8,128)S(1)}, f32[8,2,20,128]{3,0,2,1:T(8,128)S(1)}, u32[]{:S(2)}, u32[]{:S(2)}) collective-permute-start(f32[8,2,20,128]{3,0,2,1:T(8,128)S(1)} %copy.702), channel_id=1, source_target_pairs={{0,4},{4,8},{8,12},{12,16},{16,20},{20,24},{24,28},{28,32},{32,36}... | collective-permute-start | bytes 491528 | tf_op jit(solution)/shard_map/ppermute | solution.py:55
  68.1 6.0 %collective-permute-start.7 = (f32[8,2,20,128]{3,0,2,1:T(8,128)S(1)}, f32[8,2,20,128]{3,0,2,1:T(8,128)S(1)}, u32[]{:S(2)}, u32[]{:S(2)}) collective-permute-start(f32[8,2,20,128]{3,0,2,1:T(8,128)S(1)} %copy.706), channel_id=1, source_target_pairs={{4,0},{8,4},{12,8},{16,12},{20,16},{24,20},{28,24},{32,28},{36,32}... | collective-permute-start | bytes 491528 | tf_op jit(solution)/shard_map/ppermute | solution.py:56
  74.1 0.6 minimum_multiply_fusion.2
  74.7 0.3 fusion.8
  75.0 0.2 multiply_bitcast_fusion.2
  75.5 0.2 multiply_subtract_fusion
  75.9 0.8 %collective-permute-done.7 = f32[8,2,20,128]{3,0,2,1:T(8,128)S(1)} collective-permute-done((f32[8,2,20,128]{3,0,2,1:T(8,128)S(1)}, f32[8,2,20,128]{3,0,2,1:T(8,128)S(1)}, u32[]{:S(2)}, u32[]{:S(2)}) %collective-permute-start.7) | collective-permute-done | bytes 163872 | tf_op jit(solution)/shard_map/ppermute | solution.py:56
  76.7 0.1 pad_maximum_fusion.1
  77.0 0.3 minimum_multiply_fusion.4
  77.3 0.1 fusion.12
  77.4 0.1 multiply_bitcast_fusion.4
  77.9 0.2 subtract_multiply_fusion.2
  78.1 1.2 %fusion.32 = f32[8,8,16,128]{3,2,1,0:T(8,128)} fusion(f32[8,8,16,128]{3,2,1,0:T(8,128)S(1)} %copy-done, f32[8,8,16,128]{3,2,1,0:T(8,128)S(1)} %fusion.28, f32[8,8,16,128]{3,2,1,0:T(8,128)S(1)} %constant_dynamic-update-slice_fusion.55, f32[8,8,17,128]{3,2,1,0:T(8,128)S(1)} %multiply_subtract_fusion, f32[8,8,16,129]{3,2,1,0:T(8,128)S(1)} %subtract_multiply_fusion, ...), kind=kLoop, calls=%fused_computation.97 | loop fusion | flops 1703936 | bytes 5251104 | tf_op jit(solution)/shard_map/add | solution.py:228
  (166 shorter events, 5.2 us)
Async XLA Ops:
  0.6 9.4 %copy-start = (f32[8,8,16,128]{3,2,1,0:T(8,128)S(1)}, f32[8,8,16,128]{3,2,1,0:T(8,128)}, u32[]{:S(2)}) copy-start(f32[8,8,16,128]{3,2,1,0:T(8,128)} %param.2) | copy-start | bytes 1572868
  1.8 41.8 %collective-permute-start = (f32[8,8,2,128]{3,1,2,0:T(8,128)S(1)}, f32[8,8,2,128]{3,1,2,0:T(8,128)S(1)}, u32[]{:S(2)}, u32[]{:S(2)}) collective-permute-start(f32[8,8,2,128]{3,1,2,0:T(8,128)S(1)} %copy.721), channel_id=1, source_target_pairs={{0,1},{1,2},{2,3},{3,0},{4,5},{5,6},{6,7},{7,4},{8,9},{9,10},{10,1... | collective-permute-start | bytes 196616 | tf_op jit(solution)/shard_map/ppermute | solution.py:55
  3.5 40.2 %collective-permute-start.1 = (f32[8,8,2,128]{3,1,2,0:T(8,128)S(1)}, f32[8,8,2,128]{3,1,2,0:T(8,128)S(1)}, u32[]{:S(2)}, u32[]{:S(2)}) collective-permute-start(f32[8,8,2,128]{3,1,2,0:T(8,128)S(1)} %copy.722), channel_id=1, source_target_pairs={{1,0},{2,1},{3,2},{0,3},{5,4},{6,5},{7,6},{4,7},{9,8},{10,9},{11,1... | collective-permute-start | bytes 196616 | tf_op jit(solution)/shard_map/ppermute | solution.py:56
  6.7 9.9 %all-to-all-start = ((f32[4,1,8]{2,1,0:T(1,128)}), f32[4,1,8]{2,1,0:T(1,128)S(1)}, u32[]{:S(2)}, u32[]{:S(2)}) async-start(f32[4,1,8]{2,1,0:T(1,128)} %broadcast_in_dim.45), calls=%async_computation | async-start | bytes 4096 | tf_op jit(solution)/shard_map/all_to_all | solution.py:19
  18.6 20.6 %all-to-all-start.1 = ((f32[64,1,1]{2,1,0:T(1,128)}), f32[64,1,1]{2,1,0:T(1,128)S(1)}, u32[]{:S(2)}, u32[]{:S(2)}) async-start(f32[64,1,1]{2,1,0:T(1,128)} %broadcast_in_dim.46), calls=%async_computation.1 | async-start | bytes 65536 | tf_op jit(solution)/shard_map/all_to_all | solution.py:19
  44.0 6.6 %collective-permute-start.3 = (f32[8,2,20,128]{3,0,2,1:T(8,128)S(1)}, f32[8,2,20,128]{3,0,2,1:T(8,128)S(1)}, u32[]{:S(2)}, u32[]{:S(2)}) collective-permute-start(f32[8,2,20,128]{3,0,2,1:T(8,128)S(1)} %copy.686), channel_id=1, source_target_pairs={{4,0},{8,4},{12,8},{16,12},{20,16},{24,20},{28,24},{32,28},{36,32}... | collective-permute-start | bytes 491528 | tf_op jit(solution)/shard_map/ppermute | solution.py:56
  46.9 8.7 %collective-permute-start.2 = (f32[8,2,20,128]{3,0,2,1:T(8,128)S(1)}, f32[8,2,20,128]{3,0,2,1:T(8,128)S(1)}, u32[]{:S(2)}, u32[]{:S(2)}) collective-permute-start(f32[8,2,20,128]{3,0,2,1:T(8,128)S(1)} %copy.682), channel_id=1, source_target_pairs={{0,4},{4,8},{8,12},{12,16},{16,20},{20,24},{24,28},{28,32},{32,36}... | collective-permute-start | bytes 491528 | tf_op jit(solution)/shard_map/ppermute | solution.py:55
  57.9 7.8 %collective-permute-start.4 = (f32[8,8,2,128]{3,1,2,0:T(8,128)S(1)}, f32[8,8,2,128]{3,1,2,0:T(8,128)S(1)}, u32[]{:S(2)}, u32[]{:S(2)}) collective-permute-start(f32[8,8,2,128]{3,1,2,0:T(8,128)S(1)} %copy.696), channel_id=1, source_target_pairs={{0,1},{1,2},{2,3},{3,0},{4,5},{5,6},{6,7},{7,4},{8,9},{9,10},{10,1... | collective-permute-start | bytes 196616 | tf_op jit(solution)/shard_map/ppermute | solution.py:55
  60.0 5.7 %collective-permute-start.5 = (f32[8,8,2,128]{3,1,2,0:T(8,128)S(1)}, f32[8,8,2,128]{3,1,2,0:T(8,128)S(1)}, u32[]{:S(2)}, u32[]{:S(2)}) collective-permute-start(f32[8,8,2,128]{3,1,2,0:T(8,128)S(1)} %copy.697), channel_id=1, source_target_pairs={{1,0},{2,1},{3,2},{0,3},{5,4},{6,5},{7,6},{4,7},{9,8},{10,9},{11,1... | collective-permute-start | bytes 196616 | tf_op jit(solution)/shard_map/ppermute | solution.py:56
  66.1 9.7 %collective-permute-start.6 = (f32[8,2,20,128]{3,0,2,1:T(8,128)S(1)}, f32[8,2,20,128]{3,0,2,1:T(8,128)S(1)}, u32[]{:S(2)}, u32[]{:S(2)}) collective-permute-start(f32[8,2,20,128]{3,0,2,1:T(8,128)S(1)} %copy.702), channel_id=1, source_target_pairs={{0,4},{4,8},{8,12},{12,16},{16,20},{20,24},{24,28},{28,32},{32,36}... | collective-permute-start | bytes 491528 | tf_op jit(solution)/shard_map/ppermute | solution.py:55
  68.1 8.6 %collective-permute-start.7 = (f32[8,2,20,128]{3,0,2,1:T(8,128)S(1)}, f32[8,2,20,128]{3,0,2,1:T(8,128)S(1)}, u32[]{:S(2)}, u32[]{:S(2)}) collective-permute-start(f32[8,2,20,128]{3,0,2,1:T(8,128)S(1)} %copy.706), channel_id=1, source_target_pairs={{4,0},{8,4},{12,8},{16,12},{20,16},{24,20},{28,24},{32,28},{36,32}... | collective-permute-start | bytes 491528 | tf_op jit(solution)/shard_map/ppermute | solution.py:56
where the time goes:
time: 79.7 us; the launch traced here: 79.3 us
  starting transfers between devices  34.8 us (44%)
  other arithmetic  18.4 us (23%)
  waiting for transfers between devices  13.5 us (17%)
  local copies, waits for them, and re-layouts  8.12 us (10%)
  between operations  4.41 us (6%)
    all_to_all x2, starting transfers between devices, from_everyone(): lax.all_to_all(jnp.broadcast_to(value[None], (peers, *value.shape)), axis...  15.3 us
    ppermute x4, starting transfers between devices, extended_2(): after = lax.ppermute(initial, axis, down)  11.7 us
    ppermute x4, starting transfers between devices, extended_2(): before = lax.ppermute(last, axis, up)  7.77 us
    all_to_all x2, waiting for transfers between devices, from_everyone(): lax.all_to_all(jnp.broadcast_to(value[None], (peers, *value.shape)), axis...  7.71 us
    ppermute x4, waiting for transfers between devices, extended_2(): before = lax.ppermute(last, axis, up)  4.95 us
    mul x6, other arithmetic, face_flux(): 0.5 * (jnp.sign(below_diff) + jnp.sign(above_diff))  3.14 us
    unnamed x93, other arithmetic  3.07 us
    add x6, other arithmetic, face_flux(): lax.slice_in_dim(values, 1, interior + 2, axis=along_dim)  2.36 us
  transfers between devices with their start and end apart: 10, of which 3 were waited for; matrix products, arithmetic and copies ran while one was open for 25% of the time, Pallas kernels for 0%

commit v1 on v0

v1 whole, which is shorter than its diff:
```python
import math

import jax
import jax.numpy as jnp
import numpy as np
from jax import lax
from jax.experimental import pallas as pl
from jax.experimental.pallas import tpu as pltpu
from jax.sharding import PartitionSpec as P

ADIABATIC = 4.0 / 3.0
INNER_RADIUS = 1.0
OUTER_RADIUS = 2.0
COURANT = 0.4
GRAVITY_KICK = 0.004
MINIMUM_DENSITY = 0.05
PRESSURE_FLOOR = 0.01

MESH = pl.DeviceIdType.MESH
NV = 8
RD = 8
NW = 16
NT = 128
PAD = 8
ROWS = 32
XN, ZC, YN = 4, 16, 4
RADIAL = XN * ZC


def step_sizes(radial_total, phi_total, theta_total):
    theta_step = math.pi / theta_total
    phi_step = 2.0 * math.pi / phi_total
    polar_width = INNER_RADIUS * math.sin(0.5 * theta_step) * phi_step
    radial_step = min(2.0 * polar_width, (OUTER_RADIUS - INNER_RADIUS) / radial_total)
    timestep = COURANT * min(radial_step, polar_width)
    return (radial_step, theta_step, phi_step, timestep)


DR, DTH, DPH, DT = step_sizes(RADIAL * RD, YN * NW, NT)
STRENGTH = GRAVITY_KICK / DT


def polar_table():
    center = (np.arange(NT) + 0.5) * DTH
    face = np.arange(NT + 1) * DTH
    sine, face_sine = np.sin(center), np.sin(face)
    table = np.zeros((8, NT))
    table[0] = 0.5 * DT * face_sine[:-1] / (sine * DTH)
    table[1] = 0.5 * DT * face_sine[1:] / (sine * DTH)
    table[2] = 0.5 * DT / (sine * DPH)
    table[3] = np.cos(center) / sine
    table[4] = sine * (DR * DTH * DPH)
    return table.astype(np.float32)


def thermo(u):
    density = jnp.maximum(u[0], MINIMUM_DENSITY)
    inverse = 1.0 / density
    kinetic = 0.5 * (u[1] * u[1] + u[2] * u[2] + u[3] * u[3]) * inverse
    pressure = jnp.maximum((ADIABATIC - 1.0) * (u[4] - kinetic), PRESSURE_FLOOR * density)
    return density, inverse, pressure


def side(u, m):
    _, inverse, pressure = thermo(u)
    normal = u[m] * inverse
    square = ADIABATIC * pressure * inverse
    return pressure, normal, jnp.abs(normal) + square * lax.rsqrt(square)


def minmod(a, b):
    return jnp.maximum(jnp.minimum(a, b), jnp.minimum(jnp.maximum(a, b), 0.0))


def twice_flux(left, right, m):
    pl_, vl, al = side(left, m)
    pr_, vr, ar = side(right, m)
    signal = jnp.maximum(al, ar)
    cl, cr = vl + signal, vr - signal
    flux = [cl * a + cr * b for a, b in zip(left, right)]
    flux[m] = flux[m] + (pl_ + pr_)
    flux[4] = flux[4] + (pl_ * vl + pr_ * vr)
    return flux


def kernel(
    x_ref, core_ref, polar_ref, out_ref, enc_ref,
    e0, e1, acc, fp, out_v, tb, gt, enc_v, rows_src, rows_in, l1_in, l2_src, l2_in,
    load_sem, out_sem, enc_sem, h_send, h_recv, r_send, r_recv, a_send, a_recv, b_send, b_recv,
):
    r, y = lax.axis_index("radial"), lax.axis_index("phi")
    zc, xi = lax.rem(r, ZC), r // ZC
    first, last = r == 0, r == RADIAL - 1

    load = pltpu.make_async_copy(x_ref, e0.at[:, 2 : 2 + RD, PAD : PAD + NW, :], load_sem)
    load.start()

    line = [(xi * ZC + lax.rem(zc + d, ZC), y) for d in range(1, ZC)]
    wedge = [(r, lax.rem(y + d, YN)) for d in range(1, YN)]
    barrier = pltpu.get_barrier_semaphore()

    def greet(device):
        pl.semaphore_signal(barrier, inc=1, device_id=device, device_id_type=MESH)

    for device in line + wedge:
        greet(device)
    for d in range(1, XN):

        @pl.when(xi - d >= 0)
        def _(d=d):
            for yy in range(YN):
                greet((r - d * ZC, yy))

    @pl.when(jnp.logical_not(first))
    def _():
        for yy in range(YN):
            greet((r - 1, yy))

    @pl.when(jnp.logical_not(last))
    def _():
        for yy in range(YN):
            greet((r + 1, yy))

    row = lax.broadcasted_iota(jnp.int32, (16, NT), 0)
    lane = lax.broadcasted_iota(jnp.int32, (8, NT), 1)
    center = INNER_RADIUS + ((r * RD - 2 + row).astype(jnp.float32) + 0.5) * DR
    square = center * center
    below, above = center - 0.5 * DR, center + 0.5 * DR
    tb[0] = 0.5 * DT * (above * above) / (square * DR)
    tb[1] = 0.5 * DT * (below * below) / (square * DR)
    tb[2] = 1.0 / center
    tb[3] = (STRENGTH * DT) / square
    tb[4] = square

    def at(table, k):
        return tb[table, pl.ds(k + 2, 1), :]

    load.wait()

    weight = polar_ref[4:5, :]
    total = None
    for k in range(RD):
        part = e0[0, 2 + k, PAD : PAD + 8, :] + e0[0, 2 + k, PAD + 8 : PAD + 16, :]
        part = jnp.sum(part, axis=0, keepdims=True) * weight * at(4, k)
        rows_src[k : k + 1, :] = part
        total = part if total is None else total + part
    l1_in[pl.ds(zc, 1)] = total[None]
    rows_in[1, pl.ds(y, 1)] = rows_src[...][None]

    count = ZC - 1 + YN - 1 + YN * (XN - 1 - xi)
    count = count + jnp.where(first, 0, YN) + jnp.where(last, 0, YN)
    pl.semaphore_wait(barrier, count)

    def halo(e, base, which):
        phi_rows, own = pl.ds(2, RD), pl.ds(PAD, NW)
        src, dst, device = (
            (e.at[:, phi_rows, pl.ds(PAD, 2), :], e.at[:, phi_rows, pl.ds(PAD + NW, 2), :], (r, lax.rem(y + YN - 1, YN))),
            (e.at[:, phi_rows, pl.ds(PAD + NW - 2, 2), :], e.at[:, phi_rows, pl.ds(PAD - 2, 2), :], (r, lax.rem(y + 1, YN))),
            (e.at[:, pl.ds(2, 2), own, :], e.at[:, pl.ds(2 + RD, 2), own, :], (r - 1, y)),
            (e.at[:, pl.ds(RD, 2), own, :], e.at[:, pl.ds(0, 2), own, :], (r + 1, y)),
        )[which]
        return pltpu.make_async_remote_copy(
            src_ref=src, dst_ref=dst, send_sem=h_send.at[base + which], recv_sem=h_recv.at[base + which],
            device_id=device, device_id_type=MESH,
        )

    def start_halos(e, base):
        pl.when(jnp.logical_not(first))(lambda: halo(e, base, 2).start())
        pl.when(jnp.logical_not(last))(lambda: halo(e, base, 3).start())
        halo(e, base, 0).start()
        halo(e, base, 1).start()

    def wait_halos(e, base):
        pl.when(jnp.logical_not(last))(lambda: halo(e, base, 2).wait_recv())
        pl.when(jnp.logical_not(first))(lambda: halo(e, base, 3).wait_recv())
        halo(e, base, 0).wait_recv()
        halo(e, base, 1).wait_recv()

    def wait_sent(e, base):
        pl.when(jnp.logical_not(first))(lambda: halo(e, base, 2).wait_send())
        pl.when(jnp.logical_not(last))(lambda: halo(e, base, 3).wait_send())
        halo(e, base, 0).wait_send()
        halo(e, base, 1).wait_send()

    def line_copy(d):
        return pltpu.make_async_remote_copy(
            src_ref=l1_in.at[zc], dst_ref=l1_in.at[zc], send_sem=a_send.at[d], recv_sem=a_recv.at[zc],
            device_id=line[d - 1], device_id_type=MESH,
        )

    def line_arrival(d):
        j = lax.rem(zc + d, ZC)
        return pltpu.make_async_remote_copy(
            src_ref=l1_in.at[j], dst_ref=l1_in.at[j], send_sem=a_send.at[d], recv_sem=a_recv.at[j],
            device_id=line[d - 1], device_id_type=MESH,
        )

    def rows_copy(group, yy, slot, device):
        return pltpu.make_async_remote_copy(
            src_ref=rows_src, dst_ref=rows_in.at[group, slot], send_sem=r_send.at[group * YN + yy],
            recv_sem=r_recv.at[group, slot], device_id=device, device_id_type=MESH,
        )

    for d in range(1, ZC):
        line_copy(d).start()
    start_halos(e0, 0)
    for d in range(1, YN):
        rows_copy(1, d, y, wedge[d - 1]).start()

    @pl.when(jnp.logical_not(first))
    def _():
        for yy in range(YN):
            rows_copy(2, yy, y, (r - 1, yy)).start()

    @pl.when(jnp.logical_not(last))
    def _():
        for yy in range(YN):
            rows_copy(0, yy, y, (r + 1, yy)).start()

    is_first_lane = lane == 0

    def polar_part(e, k, h, gravity):
        rows = pl.ds(PAD + 8 * h, 8)
        u = [e[v, k + 2, rows, :] for v in range(NV)]
        left, right = [], []
        for v in range(NV):
            back = pltpu.roll(u[v], 1, 1)
            diff = jnp.where(is_first_lane, 0.0, u[v] - back)
            slope = 0.5 * minmod(diff, pltpu.roll(diff, NT - 1, 1))
            left.append(pltpu.roll(u[v] + slope, 1, 1))
            right.append(jnp.where(is_first_lane, back, u[v] - slope))
        flux = twice_flux(left, right, 2)
        inverse_r = at(2, k)
        low, high = polar_ref[0:1, :] * inverse_r, polar_ref[1:2, :] * inverse_r
        new = [u[v] - (pltpu.roll(flux[v], NT - 1, 1) * high - flux[v] * low) for v in range(NV)]
        density, inverse, pressure = thermo(u)
        v1, v2, v3 = u[1] * inverse, u[2] * inverse, u[3] * inverse
        cot, step_r = polar_ref[3:4, :], DT * inverse_r
        d3 = density * v3
        d33 = d3 * v3
        new[1] = new[1] + (2.0 * pressure + density * (v2 * v2) + d33) * step_r
        new[2] = new[2] + ((pressure + d33) * cot - density * v1 * v2) * step_r
        new[3] = new[3] - d3 * (v1 + v2 * cot) * step_r
        if gravity:
            pull = gt[pl.ds(k + 2, 1), :]
            new[1] = new[1] - density * pull
            new[4] = new[4] - u[1] * pull
        for v in range(NV):
            acc[v, k, pl.ds(8 * h, 8), :] = new[v]

    def polar_phase(e, gravity):
        def step(k, _):
            for h in range(2):
                polar_part(e, k, h, gravity)
            return 0

        lax.fori_loop(0, RD, step, 0)

    def radial_phase(e):
        def step(h, _):
            rows = pl.ds(pl.multiple_of(PAD + 8 * h, 8), 8)
            mine = pl.ds(pl.multiple_of(8 * h, 8), 8)
            value = [e[v, 1, rows, :] for v in range(NV)]
            diff = [value[v] - e[v, 0, rows, :] for v in range(NV)]
            left = before = None
            for k in range(-1, RD + 1):
                after = [e[v, k + 3, rows, :] for v in range(NV)]
                ahead = [after[v] - value[v] for v in range(NV)]
                slope = [0.5 * minmod(diff[v], ahead[v]) for v in range(NV)]
                if k >= 0:
                    flux = twice_flux(left, [value[v] - slope[v] for v in range(NV)], 1)
                    if k >= 1:
                        up, down = at(0, k - 1), at(1, k - 1)
                        for v in range(NV):
                            acc[v, k - 1, mine, :] = acc[v, k - 1, mine, :] - (flux[v] * up - before[v] * down)
                    before = flux
                left = [value[v] + slope[v] for v in range(NV)]
                value, diff = after, ahead
            return 0

        lax.fori_loop(0, 2, step, 0)

    def azimuth_flux(load_at):
        u = [[load_at(v, s) for v in range(NV)] for s in range(-2, 2)]
        back = [u[1][v] - u[0][v] for v in range(NV)]
        here = [u[2][v] - u[1][v] for v in range(NV)]
        ahead = [u[3][v] - u[2][v] for v in range(NV)]
        left = [u[1][v] + 0.5 * minmod(back[v], here[v]) for v in range(NV)]
        right = [u[2][v] - 0.5 * minmod(here[v], ahead[v]) for v in range(NV)]
        return twice_flux(left, right, 3)

    def azimuth_phase(e, finish):
        flat = e.reshape(NV * 12 * ROWS, NT)
        flux = azimuth_flux(
            lambda v, s: flat[pl.ds((v * 12 + 2) * ROWS + PAD + NW + s, RD, stride=ROWS), :]
        )
        fp_flat = fp.reshape(NV * RD * 24, NT)
        for v in range(NV):
            fp_flat[pl.ds(v * RD * 24 + NW, RD, stride=24), :] = flux[v]

        def step(k, _):
            for h in range(2):
                flux = azimuth_flux(lambda v, s: e[v, k + 2, PAD + 8 * h + s : PAD + 8 * h + s + 8, :])
                for v in range(NV):
                    fp[v, k, 8 * h : 8 * h + 8, :] = flux[v]
            scale = polar_ref[2:3, :] * at(2, k)
            for h in range(2):
                for v in range(NV):
                    net = fp[v, k, 8 * h + 1 : 8 * h + 9, :] - fp[v, k, 8 * h : 8 * h + 8, :]
                    finish(v, k, h, acc[v, k, 8 * h : 8 * h + 8, :] - net * scale)
            return 0

        lax.fori_loop(0, RD, step, 0)

    def edges(e):
        @pl.when(first)
        def _():
            for j in range(2):
                e[:, j, PAD : PAD + NW, :] = e[:, 2, PAD : PAD + NW, :]

        @pl.when(last)
        def _():
            for j in range(2):
                e[:, 2 + RD + j, PAD : PAD + NW, :] = e[:, 1 + RD, PAD : PAD + NW, :]

    polar_phase(e0, False)

    for d in range(1, ZC):
        line_arrival(d).wait_recv()
    whole = inner = None
    for j in range(ZC):
        part = l1_in[j]
        kept = jnp.where(j < zc, part, 0.0)
        whole = part if j == 0 else whole + part
        inner = kept if j == 0 else inner + kept
    l2_src[0:1, :] = whole
    l2_src[1:2, :] = inner
    me = xi * YN + y
    l2_in[pl.ds(me, 1)] = l2_src[...][None]

    def plane_copy(sem, slot, device):
        return pltpu.make_async_remote_copy(
            src_ref=l2_src, dst_ref=l2_in.at[slot], send_sem=b_send.at[sem], recv_sem=b_recv.at[slot],
            device_id=device, device_id_type=MESH,
        )

    for d in range(1, YN):
        plane_copy(d, me, wedge[d - 1]).start()
    for d in range(1, XN):

        @pl.when(xi + d < XN)
        def _(d=d):
            for yy in range(YN):
                plane_copy(d * YN + yy, me, (r + d * ZC, yy)).start()

    wait_halos(e0, 0)
    edges(e0)
    radial_phase(e0)

    def finish_one(v, k, h, value):
        e1[v, k + 2, PAD + 8 * h : PAD + 8 * h + 8, :] = value

    azimuth_phase(e0, finish_one)
    start_halos(e1, 4)

    for d in range(1, YN):
        j = lax.rem(y + d, YN)
        rows_copy(1, d, j, wedge[d - 1]).wait_recv()
        plane_copy(d, xi * YN + j, wedge[d - 1]).wait_recv()

    @pl.when(jnp.logical_not(first))
    def _():
        for yy in range(YN):
            rows_copy(0, yy, yy, (r - 1, yy)).wait_recv()

    @pl.when(jnp.logical_not(last))
    def _():
        for yy in range(YN):
            rows_copy(2, yy, yy, (r + 1, yy)).wait_recv()

    @pl.when(first)
    def _():
        rows_in[0] = jnp.zeros((YN, RD, NT), jnp.float32)

    @pl.when(last)
    def _():
        rows_in[2] = jnp.zeros((YN, RD, NT), jnp.float32)

    for d in range(1, XN):

        @pl.when(xi - d >= 0)
        def _(d=d):
            for yy in range(YN):
                plane_copy(0, (xi - d) * YN + yy, (r - d * ZC, yy)).wait_recv()

    base = None
    for xx in range(XN):
        for yy in range(YN):
            pair = l2_in[xx * YN + yy]
            kept = jnp.where(xx < xi, pair[0:1, :], jnp.where(xx == xi, pair[1:2, :], 0.0))
            base = kept if base is None else base + kept
    inside, own, outside = (rows_in[g, 0] + rows_in[g, 1] + rows_in[g, 2] + rows_in[g, 3] for g in range(3))
    one = [own[k : k + 1, :] for k in range(RD)]
    gt[1:2, :] = base - 0.5 * inside[7:8, :]
    gt[0:1, :] = base - inside[7:8, :] - 0.5 * inside[6:7, :]
    sofar = base
    for k in range(RD):
        gt[k + 2 : k + 3, :] = sofar + 0.5 * one[k]
        sofar = sofar + one[k]
    gt[RD + 2 : RD + 3, :] = sofar + 0.5 * outside[0:1, :]
    gt[RD + 3 : RD + 4, :] = sofar + outside[0:1, :] + 0.5 * outside[1:2, :]
    gt[RD + 4 : 16, :] = jnp.zeros((4, NT), jnp.float32)
    enclosed = jnp.broadcast_to(jnp.sum(gt[...], axis=1, keepdims=True), (16, NT)) + core_ref[0]
    diagonal = lax.broadcasted_iota(jnp.int32, (16, NT), 1) + 2 == row
    enc_v[...] = jnp.sum(jnp.where(diagonal, enclosed, 0.0), axis=0, keepdims=True)
    gt[...] = enclosed * tb[3]
    enc_out = pltpu.make_async_copy(enc_v.at[:, pl.ds(0, NT)], enc_ref, enc_sem)
    enc_out.start()

    def pull_down(k, rows):
        pull = gt[pl.ds(k + 2, 1), :]
        density = jnp.maximum(e0[0, k + 2, rows, :], MINIMUM_DENSITY)
        e1[1, k + 2, rows, :] = e1[1, k + 2, rows, :] - density * pull
        e1[4, k + 2, rows, :] = e1[4, k + 2, rows, :] - e0[1, k + 2, rows, :] * pull

    wait_sent(e1, 4)
    for k in range(RD):
        pull_down(k, pl.ds(PAD, NW))

    polar_phase(e1, True)
    wait_halos(e1, 4)
    for k in range(RD):
        pull_down(k, pl.ds(PAD - 2, 2))
        pull_down(k, pl.ds(PAD + NW, 2))
    for k in (-2, -1, RD, RD + 1):
        pull_down(k, pl.ds(PAD, NW))
    edges(e1)
    radial_phase(e1)

    def finish_two(v, k, h, value):
        out_v[v, k, 8 * h : 8 * h + 8, :] = 0.5 * (e0[v, k + 2, PAD + 8 * h : PAD + 8 * h + 8, :] + value)

    azimuth_phase(e1, finish_two)
    store = pltpu.make_async_copy(out_v, out_ref, out_sem)
    store.start()

    wait_sent(e0, 0)
    for d in range(1, ZC):
        line_copy(d).wait_send()
    for d in range(1, YN):
        rows_copy(1, d, y, wedge[d - 1]).wait_send()
        plane_copy(d, me, wedge[d - 1]).wait_send()

    @pl.when(jnp.logical_not(first))
    def _():
        for yy in range(YN):
            rows_copy(2, yy, y, (r - 1, yy)).wait_send()

    @pl.when(jnp.logical_not(last))
    def _():
        for yy in range(YN):
            rows_copy(0, yy, y, (r + 1, yy)).wait_send()

    for d in range(1, XN):

        @pl.when(xi + d < XN)
        def _(d=d):
            for yy in range(YN):
                plane_copy(d * YN + yy, me, (r + d * ZC, yy)).wait_send()

    enc_out.wait()
    store.wait()


def body(conserved, core_mass):
    f32 = jnp.float32
    dma = pltpu.SemaphoreType.DMA
    vmem = pltpu.VMEM
    extended = vmem((NV, RD + 4, ROWS, NT), f32)
    slab = vmem((NV, RD, NW, NT), f32)
    advanced, enclosed = pl.pallas_call(
        kernel,
        out_shape=(
            jax.ShapeDtypeStruct(conserved.shape, f32),
            jax.ShapeDtypeStruct((1, NT), f32),
        ),
        in_specs=[
            pl.BlockSpec(memory_space=pl.ANY),
            pl.BlockSpec(memory_space=pltpu.SMEM),
            pl.BlockSpec(memory_space=vmem),
        ],
        out_specs=(pl.BlockSpec(memory_space=pl.ANY), pl.BlockSpec(memory_space=pl.ANY)),
        scratch_shapes=[
            extended, extended, slab, vmem((NV, RD, 24, NT), f32), slab,
            vmem((5, 16, NT), f32), vmem((16, NT), f32), vmem((1, NT), f32),
            vmem((RD, NT), f32), vmem((3, YN, RD, NT), f32),
            vmem((ZC, 1, NT), f32), vmem((2, NT), f32), vmem((XN * YN, 2, NT), f32),
            dma, dma, dma, dma((8,)), dma((8,)), dma((3 * YN,)), dma((3, YN)),
            dma((ZC,)), dma((ZC,)), dma((XN * YN,)), dma((XN * YN,)),
        ],
        compiler_params=pltpu.CompilerParams(collective_id=0, has_side_effects=True),
        name="step",
    )(conserved, core_mass, jnp.asarray(polar_table()))
    return advanced, enclosed[0, :RD]


def solution(mesh):
    in_specs = (P(None, "radial", "phi", None), P())
    out_specs = (P(None, "radial", "phi", None), P("radial"))
    return jax.shard_map(body, mesh=mesh, in_specs=in_specs, out_specs=out_specs, check_vma=False)
```

time: 79.7 us -> 29.8 us (0.37)
  the two profiles are of different devices: /device:TPU:2 before, /device:TPU:1 now
where the time goes in v1:
time: 29.8 us; the launch traced here: 29.6 us
  Pallas kernels  25.2 us (85%)
  local copies, waits for them, and re-layouts  3.04 us (10%)
  between operations  1.29 us (4%)
    pallas_call x1, Pallas kernels, body(): pl.pallas_call(kernel, out_shape=(jax.ShapeDtypeStruct(conserved.shape, f...  25.2 us
    unnamed x3, local copies, waits for them, and re-layouts  2.53 us

profile of v1, /device:TPU:1, one launch (start us, length us, event | category | flops | bytes accessed | tf_op | source)
XLA Modules:
  0.0 29.6 jit_solution(12801091282759520875)
XLA Ops:
  1.3 25.2 %step.1 = (f32[8,8,16,128]{3,2,1,0:T(8,128)}, f32[1,128]{1,0:T(1,128)}) custom-call(f32[8,8,16,128]{3,2,1,0:T(8,128)} %x_ref.1, f32[1]{0:T(128)S(6)} %copy.6.core_ref, f32[8,128]{1,0:T(8,128)} %constant.2.clone.polar_ref), custom_call_target="tpu_custom_call" | custom-call | tf_op jit(solution)/shard_map/step/pallas_call | solution.py:481
  26.5 0.0 copy-start
  26.5 0.7 %copy-done = f32[1,128]{1,0:T(1,128)S(1)} copy-done((f32[1,128]{1,0:T(1,128)S(1)}, f32[1,128]{1,0:T(1,128)}, u32[]{:S(2)}) %copy-start) | copy-done | bytes 536
  27.2 0.5 %slice_bitcast_fusion = f32[8]{0:T(128)} fusion(f32[1,128]{1,0:T(1,128)S(1)} %copy-done), kind=kLoop, calls=%fused_computation | loop fusion | bytes 64 | tf_op jit(solution)/shard_map/squeeze | solution.py:504
  27.7 1.9 %copy.7 = f32[8,8,16,128]{3,2,1,0:T(8,128)} copy(f32[8,8,16,128]{3,2,1,0:T(8,128)} %get-tuple-element.8) | data formatting | bytes 1048576
Async XLA Ops:
  26.5 0.7 %copy-start = (f32[1,128]{1,0:T(1,128)S(1)}, f32[1,128]{1,0:T(1,128)}, u32[]{:S(2)}) copy-start(f32[1,128]{1,0:T(1,128)} %get-tuple-element.5) | copy-start | bytes 1540

commit v2 on v1

v2 whole, which is shorter than its diff:
```python
import math

import jax
import jax.numpy as jnp
import numpy as np
from jax import lax
from jax.experimental import pallas as pl
from jax.experimental.pallas import tpu as pltpu
from jax.sharding import PartitionSpec as P

ADIABATIC = 4.0 / 3.0
INNER_RADIUS = 1.0
OUTER_RADIUS = 2.0
COURANT = 0.4
GRAVITY_KICK = 0.004
MINIMUM_DENSITY = 0.05
PRESSURE_FLOOR = 0.01

MESH = pl.DeviceIdType.MESH
NV = 8
RD = 8
NW = 16
NT = 128
PAD = 8
ROWS = 32
XN, ZC, YN = 4, 16, 4
RADIAL = XN * ZC
VMEM_LIMIT = 24 << 20


def step_sizes(radial_total, phi_total, theta_total):
    theta_step = math.pi / theta_total
    phi_step = 2.0 * math.pi / phi_total
    polar_width = INNER_RADIUS * math.sin(0.5 * theta_step) * phi_step
    radial_step = min(2.0 * polar_width, (OUTER_RADIUS - INNER_RADIUS) / radial_total)
    timestep = COURANT * min(radial_step, polar_width)
    return (radial_step, theta_step, phi_step, timestep)


DR, DTH, DPH, DT = step_sizes(RADIAL * RD, YN * NW, NT)
STRENGTH = GRAVITY_KICK / DT


def polar_table():
    center = (np.arange(NT) + 0.5) * DTH
    face = np.arange(NT + 1) * DTH
    sine, face_sine = np.sin(center), np.sin(face)
    table = np.zeros((8, NT))
    table[0] = 0.5 * DT * face_sine[:-1] / (sine * DTH)
    table[1] = 0.5 * DT * face_sine[1:] / (sine * DTH)
    table[2] = 0.5 * DT / (sine * DPH)
    table[3] = np.cos(center) / sine
    table[4] = sine * (DR * DTH * DPH)
    return table.astype(np.float32)


def thermo(u):
    density = jnp.maximum(u[0], MINIMUM_DENSITY)
    inverse = 1.0 / density
    kinetic = 0.5 * (u[1] * u[1] + u[2] * u[2] + u[3] * u[3]) * inverse
    pressure = jnp.maximum((ADIABATIC - 1.0) * (u[4] - kinetic), PRESSURE_FLOOR * density)
    return density, inverse, pressure


def side(u, m):
    _, inverse, pressure = thermo(u)
    normal = u[m] * inverse
    square = ADIABATIC * pressure * inverse
    return pressure, normal, jnp.abs(normal) + square * lax.rsqrt(square)


def minmod(a, b):
    return jnp.maximum(jnp.minimum(a, b), jnp.minimum(jnp.maximum(a, b), 0.0))


def twice_flux(left, right, m):
    pl_, vl, al = side(left, m)
    pr_, vr, ar = side(right, m)
    signal = jnp.maximum(al, ar)
    cl, cr = vl + signal, vr - signal
    flux = [cl * a + cr * b for a, b in zip(left, right)]
    flux[m] = flux[m] + (pl_ + pr_)
    flux[4] = flux[4] + (pl_ * vl + pr_ * vr)
    return flux


def at(tb, table, k):
    return tb[table, pl.ds(k + 2, 1), :]


def polar_phase(e, acc, tb, polar, gt):
    is_first_lane = lax.broadcasted_iota(jnp.int32, (8, NT), 1) == 0

    def tile(k, h):
        u = [e[v, k + 2, PAD + 8 * h : PAD + 8 * h + 8, :] for v in range(NV)]
        left, right = [], []
        for v in range(NV):
            back = pltpu.roll(u[v], 1, 1)
            diff = jnp.where(is_first_lane, 0.0, u[v] - back)
            slope = 0.5 * minmod(diff, pltpu.roll(diff, NT - 1, 1))
            left.append(pltpu.roll(u[v] + slope, 1, 1))
            right.append(jnp.where(is_first_lane, back, u[v] - slope))
        flux = twice_flux(left, right, 2)
        inverse_r = at(tb, 2, k)
        low, high = polar[0:1, :] * inverse_r, polar[1:2, :] * inverse_r
        new = [u[v] - (pltpu.roll(flux[v], NT - 1, 1) * high - flux[v] * low) for v in range(NV)]
        density, inverse, pressure = thermo(u)
        v1, v2, v3 = u[1] * inverse, u[2] * inverse, u[3] * inverse
        cot, step_r = polar[3:4, :], DT * inverse_r
        d3 = density * v3
        d33 = d3 * v3
        new[1] = new[1] + (2.0 * pressure + density * (v2 * v2) + d33) * step_r
        new[2] = new[2] + ((pressure + d33) * cot - density * v1 * v2) * step_r
        new[3] = new[3] - d3 * (v1 + v2 * cot) * step_r
        if gt is not None:
            pull = gt[pl.ds(k + 2, 1), :]
            new[1] = new[1] - density * pull
            new[4] = new[4] - u[1] * pull
        for v in range(NV):
            acc[v, k, 8 * h : 8 * h + 8, :] = new[v]

    def step(k, _):
        for h in range(2):
            tile(k, h)
        return 0

    lax.fori_loop(0, RD, step, 0)


def radial_faces(e, rf, spans):
    def step(h, _):
        rows = pl.ds(pl.multiple_of(PAD + 8 * h, 8), 8)
        mine = pl.ds(pl.multiple_of(8 * h, 8), 8)
        for begin, end in spans:
            value = [e[v, begin + 1, rows, :] for v in range(NV)]
            diff = [value[v] - e[v, begin, rows, :] for v in range(NV)]
            left = None
            for k in range(begin - 1, end):
                after = [e[v, k + 3, rows, :] for v in range(NV)]
                ahead = [after[v] - value[v] for v in range(NV)]
                slope = [0.5 * minmod(diff[v], ahead[v]) for v in range(NV)]
                if k >= begin:
                    flux = twice_flux(left, [value[v] - slope[v] for v in range(NV)], 1)
                    for v in range(NV):
                        rf[v, k, mine, :] = flux[v]
                left = [value[v] + slope[v] for v in range(NV)]
                value, diff = after, ahead
        return 0

    lax.fori_loop(0, 2, step, 0)


def azimuth_flux(load_at):
    u = [[load_at(v, s) for v in range(NV)] for s in range(-2, 2)]
    back = [u[1][v] - u[0][v] for v in range(NV)]
    here = [u[2][v] - u[1][v] for v in range(NV)]
    ahead = [u[3][v] - u[2][v] for v in range(NV)]
    left = [u[1][v] + 0.5 * minmod(back[v], here[v]) for v in range(NV)]
    right = [u[2][v] - 0.5 * minmod(here[v], ahead[v]) for v in range(NV)]
    return twice_flux(left, right, 3)


def azimuth_inner(e, fp):
    def step(k, _):
        for face in (2, 7):
            flux = azimuth_flux(lambda v, s: e[v, k + 2, PAD + face + s : PAD + face + s + 8, :])
            for v in range(NV):
                fp[v, k, face : face + 8, :] = flux[v]
        return 0

    lax.fori_loop(0, RD, step, 0)


def azimuth_outer(e, fp):
    flat = e.reshape(NV * 12 * ROWS, NT)
    fp_flat = fp.reshape(NV * RD * 24, NT)
    for face in (0, 1, NW - 1, NW):
        flux = azimuth_flux(
            lambda v, s: flat[pl.ds((v * 12 + 2) * ROWS + PAD + face + s, RD, stride=ROWS), :]
        )
        for v in range(NV):
            fp_flat[pl.ds(v * RD * 24 + face, RD, stride=24), :] = flux[v]


def finish_zones(acc, rf, fp, tb, polar, put, row_done):
    for k in range(RD):
        up, down = at(tb, 0, k), at(tb, 1, k)
        scale = polar[2:3, :] * at(tb, 2, k)
        for h in range(2):
            mine = slice(8 * h, 8 * h + 8)
            for v in range(NV):
                radial = rf[v, k + 1, mine, :] * up - rf[v, k, mine, :] * down
                azimuth = (fp[v, k, 8 * h + 1 : 8 * h + 9, :] - fp[v, k, mine, :]) * scale
                put(v, k, h, acc[v, k, mine, :] - radial - azimuth)
        if row_done is not None:
            row_done(k)


def kernel(
    x_ref, core_ref, polar_hbm, e0, acc, rf, fp, tb, polar, enc_v,
    e1, gt, rows_src, rows_in, l1_in, l2_src, l2_in,
    load_sem, h_send, h_recv, r_send, r_recv, a_send, a_recv, b_send, b_recv,
):
    r, y = lax.axis_index("radial"), lax.axis_index("phi")
    zc, xi = lax.rem(r, ZC), r // ZC
    first, last = r == 0, r == RADIAL - 1
    inner_there, outer_there = jnp.logical_not(first), jnp.logical_not(last)

    load = pltpu.make_async_copy(x_ref, e0.at[:, 2 : 2 + RD, PAD : PAD + NW, :], load_sem.at[0])
    polar_load = pltpu.make_async_copy(polar_hbm, polar, load_sem.at[1])
    load.start()
    polar_load.start()

    line = [(xi * ZC + lax.rem(zc + d, ZC), y) for d in range(1, ZC)]
    wedge = [(r, lax.rem(y + d, YN)) for d in range(1, YN)]
    barrier = pltpu.get_barrier_semaphore()

    def greet(device):
        pl.semaphore_signal(barrier, inc=1, device_id=device, device_id_type=MESH)

    for device in line + wedge:
        greet(device)

    def greet_all(slab):
        for yy in range(YN):
            greet((slab, yy))

    for d in range(1, XN):
        pl.when(xi - d >= 0)(lambda d=d: greet_all(r - d * ZC))
    pl.when(inner_there)(lambda: greet_all(r - 1))
    pl.when(outer_there)(lambda: greet_all(r + 1))

    row = lax.broadcasted_iota(jnp.int32, (16, NT), 0)
    center = INNER_RADIUS + ((r * RD - 2 + row).astype(jnp.float32) + 0.5) * DR
    square = center * center
    below, above = center - 0.5 * DR, center + 0.5 * DR
    tb[0] = 0.5 * DT * (above * above) / (square * DR)
    tb[1] = 0.5 * DT * (below * below) / (square * DR)
    tb[2] = 1.0 / center
    tb[3] = (STRENGTH * DT) / square
    tb[4] = square

    polar_load.wait()
    load.wait()

    weight = polar[4:5, :]
    total = None
    for k in range(RD):
        part = e0[0, 2 + k, PAD : PAD + 8, :] + e0[0, 2 + k, PAD + 8 : PAD + 16, :]
        part = jnp.sum(part, axis=0, keepdims=True) * weight * at(tb, 4, k)
        rows_src[k : k + 1, :] = part
        total = part if total is None else total + part
    l1_in[pl.ds(zc, 1)] = total[None]
    rows_in[1, pl.ds(y, 1)] = rows_src[...][None]

    count = ZC - 1 + YN - 1 + YN * (XN - 1 - xi)
    count = count + jnp.where(first, 0, YN) + jnp.where(last, 0, YN)
    pl.semaphore_wait(barrier, count)

    def remote(src, dst, send, recv, device):
        return pltpu.make_async_remote_copy(
            src_ref=src, dst_ref=dst, send_sem=send, recv_sem=recv, device_id=device, device_id_type=MESH
        )

    def halo(e, base, which):
        phi_rows, own = pl.ds(2, RD), pl.ds(PAD, NW)
        src, dst, device = (
            (e.at[:, phi_rows, pl.ds(PAD, 2), :], e.at[:, phi_rows, pl.ds(PAD + NW, 2), :], (r, lax.rem(y + YN - 1, YN))),
            (e.at[:, phi_rows, pl.ds(PAD + NW - 2, 2), :], e.at[:, phi_rows, pl.ds(PAD - 2, 2), :], (r, lax.rem(y + 1, YN))),
            (e.at[:, pl.ds(2, 2), own, :], e.at[:, pl.ds(2 + RD, 2), own, :], (r - 1, y)),
            (e.at[:, pl.ds(RD, 2), own, :], e.at[:, pl.ds(0, 2), own, :], (r + 1, y)),
        )[which]
        return remote(src, dst, h_send.at[base + which], h_recv.at[base + which], device)

    def start_halos(e, base):
        pl.when(inner_there)(lambda: halo(e, base, 2).start())
        pl.when(outer_there)(lambda: halo(e, base, 3).start())
        halo(e, base, 0).start()
        halo(e, base, 1).start()

    def wait_halos(e, base):
        pl.when(outer_there)(lambda: halo(e, base, 2).wait_recv())
        pl.when(inner_there)(lambda: halo(e, base, 3).wait_recv())
        halo(e, base, 0).wait_recv()
        halo(e, base, 1).wait_recv()

    def wait_sent(e, base):
        pl.when(inner_there)(lambda: halo(e, base, 2).wait_send())
        pl.when(outer_there)(lambda: halo(e, base, 3).wait_send())
        halo(e, base, 0).wait_send()
        halo(e, base, 1).wait_send()

    def line_copy(d):
        return remote(l1_in.at[zc], l1_in.at[zc], a_send.at[d], a_recv.at[zc], line[d - 1])

    def line_arrival(d):
        j = lax.rem(zc + d, ZC)
        return remote(l1_in.at[j], l1_in.at[j], a_send.at[d], a_recv.at[j], line[d - 1])

    def rows_copy(group, sem, slot, device):
        return remote(rows_src, rows_in.at[group, slot], r_send.at[group * YN + sem], r_recv.at[group, slot], device)

    for d in range(1, ZC):
        line_copy(d).start()
    start_halos(e0, 0)
    for d in range(1, YN):
        rows_copy(1, d, y, wedge[d - 1]).start()

    def each_wedge(act):
        for yy in range(YN):
            act(yy)

    pl.when(inner_there)(lambda: each_wedge(lambda yy: rows_copy(2, yy, y, (r - 1, yy)).start()))
    pl.when(outer_there)(lambda: each_wedge(lambda yy: rows_copy(0, yy, y, (r + 1, yy)).start()))

    def edges(e):
        @pl.when(first)
        def _():
            for j in range(2):
                e[:, j, PAD : PAD + NW, :] = e[:, 2, PAD : PAD + NW, :]

        @pl.when(last)
        def _():
            for j in range(2):
                e[:, 2 + RD + j, PAD : PAD + NW, :] = e[:, 1 + RD, PAD : PAD + NW, :]

    polar_phase(e0, acc, tb, polar, None)
    radial_faces(e0, rf, ((2, RD - 1),))
    azimuth_inner(e0, fp)

    for d in range(1, ZC):
        line_arrival(d).wait_recv()
    whole = inner = None
    for j in range(ZC):
        part = l1_in[j]
        kept = jnp.where(j < zc, part, 0.0)
        whole = part if j == 0 else whole + part
        inner = kept if j == 0 else inner + kept
    l2_src[0:1, :] = whole
    l2_src[1:2, :] = inner
    me = xi * YN + y
    l2_in[pl.ds(me, 1)] = l2_src[...][None]

    def plane_copy(sem, slot, device):
        return remote(l2_src, l2_in.at[slot], b_send.at[sem], b_recv.at[slot], device)

    for d in range(1, YN):
        plane_copy(d, me, wedge[d - 1]).start()
    for d in range(1, XN):
        pl.when(xi + d < XN)(
            lambda d=d: each_wedge(lambda yy: plane_copy(d * YN + yy, me, (r + d * ZC, yy)).start())
        )

    wait_halos(e0, 0)
    edges(e0)
    radial_faces(e0, rf, ((0, 2), (RD - 1, RD + 1)))
    azimuth_outer(e0, fp)

    def put(v, k, h, value):
        e1[v, k + 2, PAD + 8 * h : PAD + 8 * h + 8, :] = value

    finish_zones(acc, rf, fp, tb, polar, put, None)
    start_halos(e1, 4)

    for d in range(1, YN):
        j = lax.rem(y + d, YN)
        rows_copy(1, d, j, wedge[d - 1]).wait_recv()
        plane_copy(d, xi * YN + j, wedge[d - 1]).wait_recv()
    pl.when(inner_there)(lambda: each_wedge(lambda yy: rows_copy(0, yy, yy, (r - 1, yy)).wait_recv()))
    pl.when(outer_there)(lambda: each_wedge(lambda yy: rows_copy(2, yy, yy, (r + 1, yy)).wait_recv()))

    @pl.when(first)
    def _():
        rows_in[0] = jnp.zeros((YN, RD, NT), jnp.float32)

    @pl.when(last)
    def _():
        rows_in[2] = jnp.zeros((YN, RD, NT), jnp.float32)

    for d in range(1, XN):
        pl.when(xi - d >= 0)(
            lambda d=d: each_wedge(
                lambda yy: plane_copy(0, (xi - d) * YN + yy, (r - d * ZC, yy)).wait_recv()
            )
        )

    base = None
    for xx in range(XN):
        for yy in range(YN):
            pair = l2_in[xx * YN + yy]
            kept = jnp.where(xx < xi, pair[0:1, :], jnp.where(xx == xi, pair[1:2, :], 0.0))
            base = kept if base is None else base + kept
    inside, own, outside = (rows_in[g, 0] + rows_in[g, 1] + rows_in[g, 2] + rows_in[g, 3] for g in range(3))
    one = [own[k : k + 1, :] for k in range(RD)]
    gt[1:2, :] = base - 0.5 * inside[7:8, :]
    gt[0:1, :] = base - inside[7:8, :] - 0.5 * inside[6:7, :]
    sofar = base
    for k in range(RD):
        gt[k + 2 : k + 3, :] = sofar + 0.5 * one[k]
        sofar = sofar + one[k]
    gt[RD + 2 : RD + 3, :] = sofar + 0.5 * outside[0:1, :]
    gt[RD + 3 : RD + 4, :] = sofar + outside[0:1, :] + 0.5 * outside[1:2, :]
    gt[RD + 4 : 16, :] = jnp.zeros((4, NT), jnp.float32)
    enclosed = jnp.broadcast_to(jnp.sum(gt[...], axis=1, keepdims=True), (16, NT)) + core_ref[0]
    diagonal = lax.broadcasted_iota(jnp.int32, (16, NT), 1) + 2 == row
    enc_v[...] = jnp.sum(jnp.where(diagonal, enclosed, 0.0), axis=0, keepdims=True)
    gt[...] = enclosed * tb[3]

    def pull_down(k, rows):
        pull = gt[pl.ds(k + 2, 1), :]
        density = jnp.maximum(e0[0, k + 2, rows, :], MINIMUM_DENSITY)
        e1[1, k + 2, rows, :] = e1[1, k + 2, rows, :] - density * pull
        e1[4, k + 2, rows, :] = e1[4, k + 2, rows, :] - e0[1, k + 2, rows, :] * pull

    wait_sent(e1, 4)
    for k in range(RD):
        pull_down(k, pl.ds(PAD, NW))

    polar_phase(e1, acc, tb, polar, gt)
    radial_faces(e1, rf, ((2, RD - 1),))
    azimuth_inner(e1, fp)
    wait_halos(e1, 4)
    for k in range(RD):
        pull_down(k, pl.ds(PAD - 2, 2))
        pull_down(k, pl.ds(PAD + NW, 2))
    for k in (-2, -1, RD, RD + 1):
        pull_down(k, pl.ds(PAD, NW))
    edges(e1)
    radial_faces(e1, rf, ((0, 2), (RD - 1, RD + 1)))
    azimuth_outer(e1, fp)

    wait_sent(e0, 0)
    for d in range(1, ZC):
        line_copy(d).wait_send()
    for d in range(1, YN):
        rows_copy(1, d, y, wedge[d - 1]).wait_send()
        plane_copy(d, me, wedge[d - 1]).wait_send()
    pl.when(inner_there)(lambda: each_wedge(lambda yy: rows_copy(2, yy, y, (r - 1, yy)).wait_send()))
    pl.when(outer_there)(lambda: each_wedge(lambda yy: rows_copy(0, yy, y, (r + 1, yy)).wait_send()))
    for d in range(1, XN):
        pl.when(xi + d < XN)(
            lambda d=d: each_wedge(lambda yy: plane_copy(d * YN + yy, me, (r + d * ZC, yy)).wait_send())
        )


def last_kernel(e0, acc, rf, fp, tb, polar, enc_v, out_ref, enc_ref, out_v, sem):
    enc_ref[...] = enc_v[0, :][:RD]

    def put(v, k, h, value):
        out_v[v, k, 8 * h : 8 * h + 8, :] = 0.5 * (e0[v, k + 2, PAD + 8 * h : PAD + 8 * h + 8, :] + value)

    def store(k):
        return pltpu.make_async_copy(out_v.at[:, k], out_ref.at[:, k], sem.at[k])

    finish_zones(acc, rf, fp, tb, polar, put, lambda k: store(k).start())
    for k in range(RD):
        store(k).wait()


def body(conserved, core_mass):
    f32 = jnp.float32
    dma = pltpu.SemaphoreType.DMA
    vmem, anywhere = pltpu.VMEM, pl.BlockSpec(memory_space=pl.ANY)
    resident = pl.BlockSpec(memory_space=vmem)
    polar = pltpu.with_memory_space_constraint(jnp.asarray(polar_table()), pltpu.HBM)
    conserved = pltpu.with_memory_space_constraint(conserved, pltpu.HBM)
    extended = vmem((NV, RD + 4, ROWS, NT), f32)
    slab = vmem((NV, RD, NW, NT), f32)
    radial_flux, azimuth_fluxes = vmem((NV, RD + 1, NW, NT), f32), vmem((NV, RD, 24, NT), f32)
    held = pl.pallas_call(
        kernel,
        out_shape=(
            extended, slab, radial_flux, azimuth_fluxes, vmem((5, 16, NT), f32), vmem((8, NT), f32), vmem((1, NT), f32),
        ),
        in_specs=[anywhere, pl.BlockSpec(memory_space=pltpu.SMEM), anywhere],
        out_specs=(resident,) * 7,
        scratch_shapes=[
            extended, vmem((16, NT), f32),
            vmem((RD, NT), f32), vmem((3, YN, RD, NT), f32),
            vmem((ZC, 1, NT), f32), vmem((2, NT), f32), vmem((XN * YN, 2, NT), f32),
            dma((2,)), dma((8,)), dma((8,)), dma((3 * YN,)), dma((3, YN)),
            dma((ZC,)), dma((ZC,)), dma((XN * YN,)), dma((XN * YN,)),
        ],
        compiler_params=pltpu.CompilerParams(
            collective_id=0, has_side_effects=True, vmem_limit_bytes=VMEM_LIMIT
        ),
        name="two_sections",
    )(conserved, core_mass, polar)
    e0, acc, rf, fp, tb, polar, enc_v = (pltpu.with_memory_space_constraint(a, vmem) for a in held)
    return pl.pallas_call(
        last_kernel,
        out_shape=(jax.ShapeDtypeStruct(conserved.shape, f32), jax.ShapeDtypeStruct((RD,), f32)),
        in_specs=[resident] * 7,
        out_specs=(anywhere, resident),
        scratch_shapes=[slab, dma((RD,))],
        compiler_params=pltpu.CompilerParams(vmem_limit_bytes=VMEM_LIMIT),
        name="last_faces",
    )(e0, acc, rf, fp, tb, polar, enc_v)


def solution(mesh):
    in_specs = (P(None, "radial", "phi", None), P())
    out_specs = (P(None, "radial", "phi", None), P("radial"))
    return jax.shard_map(body, mesh=mesh, in_specs=in_specs, out_specs=out_specs, check_vma=False)
```

time: 29.8 us -> 26.4 us (0.89)
  local copies, waits for them, and re-layouts: 3.04 us -> 0 us
    unnamed x3 -> x0, local copies, waits for them, and re-layouts: 2.53 us -> none
    squeeze x1 -> x0, local copies, waits for them, and re-layouts: 0.51 us -> none  [body(): return (advanced, enclosed[0, :RD])]
    pallas_call x1 -> x2, Pallas kernels: 25.2 us -> 25 us  [the longest x1 23.6 us: body(): pl.pallas_call(kernel, out_shape=(extended, slab, radial_flux, azimuth_fl...]
where the time goes in v2:
time: 26.4 us; the launch traced here: 26.3 us
  Pallas kernels  25 us (95%)
  between operations  1.28 us (5%)
    pallas_call x1, Pallas kernels, body(): pl.pallas_call(kernel, out_shape=(extended, slab, radial_flux, azimuth_fl...  23.6 us
    pallas_call x1, Pallas kernels, body(): pl.pallas_call(last_kernel, out_shape=(jax.ShapeDtypeStruct(conserved.sha...  1.39 us

profile of v2, /device:TPU:1, one launch (start us, length us, event | category | flops | bytes accessed | tf_op | source)
XLA Modules:
  0.0 26.3 jit_solution(2783886875714735719)
XLA Ops:
  1.3 23.6 %two_sections.1 = (f32[8,12,32,128]{3,2,1,0:T(8,128)S(1)}, f32[8,8,16,128]{3,2,1,0:T(8,128)S(1)}, f32[8,9,16,128]{3,2,1,0:T(8,128)S(1)}, f32[8,8,24,128]{3,2,1,0...) custom-call(f32[8,8,16,128]{3,2,1,0:T(8,128)} %x_ref.1, f32[1]{0:T(128)S(6)} %copy.5.core_ref, ...), custom_call_target="tpu_custom_call" | custom-call | tf_op jit(solution)/shard_map/two_sections/pallas_call | solution.py:470
  24.9 1.4 %last_faces.1 = (f32[8,8,16,128]{3,2,1,0:T(8,128)}, f32[8]{0:T(128)}) custom-call(f32[8,12,32,128]{3,2,1,0:T(8,128)S(1)} %get-tuple-element.9.e0, f32[8,8,16,128]{3,2,1,0:T(8,128)S(1)} %get-tuple-element.10.acc, f32[8,9,16,128]{3,2,1,0:T(8,128)S(1)} %get-tuple-element.11.rf, f32[8,8,24,128]{3,2,1,0:T(8,128)S(1)} %get-tuple-element.12.fp, ...), custom_call_target="tpu_custom_call" | custom-call | tf_op jit(solution)/shard_map/last_faces/pallas_call | solution.py:490

commit v3 on v2

--- a/solution.py
+++ b/solution.py
@@ -124,7 +124,7 @@
             tile(k, h)
         return 0
 
-    lax.fori_loop(0, RD, step, 0)
+    lax.fori_loop(0, RD, step, 0, unroll=4)
 
 
 def radial_faces(e, rf, spans):
@@ -198,8 +198,8 @@
 
 def kernel(
     x_ref, core_ref, polar_hbm, e0, acc, rf, fp, tb, polar, enc_v,
-    e1, gt, rows_src, rows_in, l1_in, l2_src, l2_in,
-    load_sem, h_send, h_recv, r_send, r_recv, a_send, a_recv, b_send, b_recv,
+    e1, gt, rows_src, rows_in, l1_in, wedge_src, wedge_in, plane_src, plane_in,
+    load_sem, h_send, h_recv, r_send, r_recv, a_send, a_recv, w_send, w_recv, b_send, b_recv, here_sem,
 ):
     r, y = lax.axis_index("radial"), lax.axis_index("phi")
     zc, xi = lax.rem(r, ZC), r // ZC
@@ -218,17 +218,11 @@
     def greet(device):
         pl.semaphore_signal(barrier, inc=1, device_id=device, device_id_type=MESH)
 
-    for device in line + wedge:
+    across = [(lax.rem(xi + d, XN) * ZC + zc, y) for d in range(1, XN)]
+    for device in line + wedge + across:
         greet(device)
-
-    def greet_all(slab):
-        for yy in range(YN):
-            greet((slab, yy))
-
-    for d in range(1, XN):
-        pl.when(xi - d >= 0)(lambda d=d: greet_all(r - d * ZC))
-    pl.when(inner_there)(lambda: greet_all(r - 1))
-    pl.when(outer_there)(lambda: greet_all(r + 1))
+    pl.when(inner_there)(lambda: greet((r - 1, y)))
+    pl.when(outer_there)(lambda: greet((r + 1, y)))
 
     row = lax.broadcasted_iota(jnp.int32, (16, NT), 0)
     center = INNER_RADIUS + ((r * RD - 2 + row).astype(jnp.float32) + 0.5) * DR
@@ -251,10 +245,8 @@
         rows_src[k : k + 1, :] = part
         total = part if total is None else total + part
     l1_in[pl.ds(zc, 1)] = total[None]
-    rows_in[1, pl.ds(y, 1)] = rows_src[...][None]
-
-    count = ZC - 1 + YN - 1 + YN * (XN - 1 - xi)
-    count = count + jnp.where(first, 0, YN) + jnp.where(last, 0, YN)
+
+    count = ZC - 1 + YN - 1 + XN - 1 + jnp.where(first, 0, 1) + jnp.where(last, 0, 1)
     pl.semaphore_wait(barrier, count)
 
     def remote(src, dst, send, recv, device):
@@ -293,25 +285,25 @@
     def line_copy(d):
         return remote(l1_in.at[zc], l1_in.at[zc], a_send.at[d], a_recv.at[zc], line[d - 1])
 
-    def line_arrival(d):
-        j = lax.rem(zc + d, ZC)
-        return remote(l1_in.at[j], l1_in.at[j], a_send.at[d], a_recv.at[j], line[d - 1])
-
-    def rows_copy(group, sem, slot, device):
-        return remote(rows_src, rows_in.at[group, slot], r_send.at[group * YN + sem], r_recv.at[group, slot], device)
+    def line_sum(begin, end, start):
+        def add(j, so_far):
+            remote(l1_in.at[j], l1_in.at[j], a_send.at[0], a_recv.at[j], line[0]).wait_recv()
+            return so_far + l1_in[j]
+
+        return lax.fori_loop(begin, end, add, start)
+
+    def rows_copy(group, device):
+        return remote(rows_src, rows_in.at[group], r_send.at[group], r_recv.at[group], device)
 
     for d in range(1, ZC):
         line_copy(d).start()
+    for d in range(1, XN):
+        pl.when(xi - d >= 0)(
+            lambda d=d: pl.semaphore_signal(here_sem, inc=1, device_id=(r - d * ZC, y), device_id_type=MESH)
+        )
     start_halos(e0, 0)
-    for d in range(1, YN):
-        rows_copy(1, d, y, wedge[d - 1]).start()
-
-    def each_wedge(act):
-        for yy in range(YN):
-            act(yy)
-
-    pl.when(inner_there)(lambda: each_wedge(lambda yy: rows_copy(2, yy, y, (r - 1, yy)).start()))
-    pl.when(outer_there)(lambda: each_wedge(lambda yy: rows_copy(0, yy, y, (r + 1, yy)).start()))
+    pl.when(inner_there)(lambda: rows_copy(1, (r - 1, y)).start())
+    pl.when(outer_there)(lambda: rows_copy(0, (r + 1, y)).start())
 
     def edges(e):
         @pl.when(first)
@@ -328,24 +320,40 @@
     radial_faces(e0, rf, ((2, RD - 1),))
     azimuth_inner(e0, fp)
 
-    for d in range(1, ZC):
-        line_arrival(d).wait_recv()
-    whole = inner = None
-    for j in range(ZC):
-        part = l1_in[j]
-        kept = jnp.where(j < zc, part, 0.0)
-        whole = part if j == 0 else whole + part
-        inner = kept if j == 0 else inner + kept
-    l2_src[0:1, :] = whole
-    l2_src[1:2, :] = inner
+    inner = line_sum(0, zc, jnp.zeros((1, NT), jnp.float32))
+    pl.when(inner_there)(lambda: rows_copy(0, (r - 1, y)).wait_recv())
+    pl.when(outer_there)(lambda: rows_copy(1, (r + 1, y)).wait_recv())
+
+    @pl.when(first)
+    def _():
+        rows_in[0] = jnp.zeros((RD, NT), jnp.float32)
+
+    @pl.when(last)
+    def _():
+        rows_in[1] = jnp.zeros((RD, NT), jnp.float32)
+
+    wedge_src[0:RD, :] = rows_src[...]
+    wedge_src[8:9, :] = inner
+    wedge_src[9:11, :] = rows_in[0, RD - 2 : RD, :]
+    wedge_src[11:13, :] = rows_in[1, 0:2, :]
+    wedge_src[13:16, :] = jnp.zeros((3, NT), jnp.float32)
+
+    def wedge_copy(d, slot):
+        return remote(wedge_src, wedge_in.at[slot], w_send.at[d], w_recv.at[slot], wedge[d - 1])
+
+    def plane_copy(sem, slot, device):
+        return remote(plane_src, plane_in.at[slot], b_send.at[sem], b_recv.at[slot], device)
+
+    for d in range(1, YN):
+        wedge_copy(d, y).start()
+    plane_src[...] = line_sum(zc + 1, ZC, inner + total)
+    pl.when(xi < XN - 1)(lambda: pl.semaphore_wait(here_sem, XN - 1 - xi))
+
+    def each_wedge(act):
+        for yy in range(YN):
+            act(yy)
+
     me = xi * YN + y
-    l2_in[pl.ds(me, 1)] = l2_src[...][None]
-
-    def plane_copy(sem, slot, device):
-        return remote(l2_src, l2_in.at[slot], b_send.at[sem], b_recv.at[slot], device)
-
-    for d in range(1, YN):
-        plane_copy(d, me, wedge[d - 1]).start()
     for d in range(1, XN):
         pl.when(xi + d < XN)(
             lambda d=d: each_wedge(lambda yy: plane_copy(d * YN + yy, me, (r + d * ZC, yy)).start())
@@ -362,38 +370,21 @@
     finish_zones(acc, rf, fp, tb, polar, put, None)
     start_halos(e1, 4)
 
+    parts = wedge_src[...]
     for d in range(1, YN):
         j = lax.rem(y + d, YN)
-        rows_copy(1, d, j, wedge[d - 1]).wait_recv()
-        plane_copy(d, xi * YN + j, wedge[d - 1]).wait_recv()
-    pl.when(inner_there)(lambda: each_wedge(lambda yy: rows_copy(0, yy, yy, (r - 1, yy)).wait_recv()))
-    pl.when(outer_there)(lambda: each_wedge(lambda yy: rows_copy(2, yy, yy, (r + 1, yy)).wait_recv()))
-
-    @pl.when(first)
-    def _():
-        rows_in[0] = jnp.zeros((YN, RD, NT), jnp.float32)
-
-    @pl.when(last)
-    def _():
-        rows_in[2] = jnp.zeros((YN, RD, NT), jnp.float32)
-
-    for d in range(1, XN):
-        pl.when(xi - d >= 0)(
-            lambda d=d: each_wedge(
-                lambda yy: plane_copy(0, (xi - d) * YN + yy, (r - d * ZC, yy)).wait_recv()
-            )
-        )
-
-    base = None
-    for xx in range(XN):
-        for yy in range(YN):
-            pair = l2_in[xx * YN + yy]
-            kept = jnp.where(xx < xi, pair[0:1, :], jnp.where(xx == xi, pair[1:2, :], 0.0))
-            base = kept if base is None else base + kept
-    inside, own, outside = (rows_in[g, 0] + rows_in[g, 1] + rows_in[g, 2] + rows_in[g, 3] for g in range(3))
+        wedge_copy(d, j).wait_recv()
+        parts = parts + wedge_in[j]
+
+    def plane_sum(j, so_far):
+        plane_copy(0, j, wedge[0]).wait_recv()
+        return so_far + plane_in[j]
+
+    base = lax.fori_loop(0, xi * YN, plane_sum, parts[8:9, :])
+    own, inside, outside = parts[0:RD, :], parts[9:11, :], parts[11:13, :]
     one = [own[k : k + 1, :] for k in range(RD)]
-    gt[1:2, :] = base - 0.5 * inside[7:8, :]
-    gt[0:1, :] = base - inside[7:8, :] - 0.5 * inside[6:7, :]
+    gt[1:2, :] = base - 0.5 * inside[1:2, :]
+    gt[0:1, :] = base - inside[1:2, :] - 0.5 * inside[0:1, :]
     sofar = base
     for k in range(RD):
         gt[k + 2 : k + 3, :] = sofar + 0.5 * one[k]
@@ -433,10 +424,9 @@
     for d in range(1, ZC):
         line_copy(d).wait_send()
     for d in range(1, YN):
-        rows_copy(1, d, y, wedge[d - 1]).wait_send()
-        plane_copy(d, me, wedge[d - 1]).wait_send()
-    pl.when(inner_there)(lambda: each_wedge(lambda yy: rows_copy(2, yy, y, (r - 1, yy)).wait_send()))
-    pl.when(outer_there)(lambda: each_wedge(lambda yy: rows_copy(0, yy, y, (r + 1, yy)).wait_send()))
+        wedge_copy(d, y).wait_send()
+    pl.when(inner_there)(lambda: rows_copy(1, (r - 1, y)).wait_send())
+    pl.when(outer_there)(lambda: rows_copy(0, (r + 1, y)).wait_send())
     for d in range(1, XN):
         pl.when(xi + d < XN)(
             lambda d=d: each_wedge(lambda yy: plane_copy(d * YN + yy, me, (r + d * ZC, yy)).wait_send())
@@ -476,10 +466,10 @@
         out_specs=(resident,) * 7,
         scratch_shapes=[
             extended, vmem((16, NT), f32),
-            vmem((RD, NT), f32), vmem((3, YN, RD, NT), f32),
-            vmem((ZC, 1, NT), f32), vmem((2, NT), f32), vmem((XN * YN, 2, NT), f32),
-            dma((2,)), dma((8,)), dma((8,)), dma((3 * YN,)), dma((3, YN)),
-            dma((ZC,)), dma((ZC,)), dma((XN * YN,)), dma((XN * YN,)),
+            vmem((RD, NT), f32), vmem((2, RD, NT), f32), vmem((ZC, 1, NT), f32),
+            vmem((16, NT), f32), vmem((YN, 16, NT), f32), vmem((1, NT), f32), vmem((XN * YN, 1, NT), f32),
+            dma((2,)), dma((8,)), dma((8,)), dma((2,)), dma((2,)), dma((ZC,)), dma((ZC,)),
+            dma((YN,)), dma((YN,)), dma((XN * YN,)), dma((XN * YN,)), pltpu.SemaphoreType.REGULAR,
         ],
         compiler_params=pltpu.CompilerParams(
             collective_id=0, has_side_effects=True, vmem_limit_bytes=VMEM_LIMIT

time: 26.4 us -> 23.1 us (0.88)
  Pallas kernels: 25 us -> 21.4 us
    pallas_call x1, Pallas kernels: 23.6 us -> 20.1 us  [body(): pl.pallas_call(kernel, out_shape=(extended, slab, radial_flux, azimuth_fl...]
where the time goes in v3:
time: 23.1 us; the launch traced here: 22.7 us
  Pallas kernels  21.4 us (93%)
  between operations  1.28 us (6%)
    pallas_call x1, Pallas kernels, body(): pl.pallas_call(kernel, out_shape=(extended, slab, radial_flux, azimuth_fl...  20.1 us
    pallas_call x1, Pallas kernels, body(): pl.pallas_call(last_kernel, out_shape=(jax.ShapeDtypeStruct(conserved.sha...  1.39 us

profile of v3, /device:TPU:1, one launch (start us, length us, event | category | flops | bytes accessed | tf_op | source)
XLA Modules:
  0.0 22.7 jit_solution(18203303162575516531)
XLA Ops:
  1.3 20.1 %two_sections.1 = (f32[8,12,32,128]{3,2,1,0:T(8,128)S(1)}, f32[8,8,16,128]{3,2,1,0:T(8,128)S(1)}, f32[8,9,16,128]{3,2,1,0:T(8,128)S(1)}, f32[8,8,24,128]{3,2,1,0...) custom-call(f32[8,8,16,128]{3,2,1,0:T(8,128)} %x_ref.1, f32[1]{0:T(128)S(6)} %copy.5.core_ref, ...), custom_call_target="tpu_custom_call" | custom-call | tf_op jit(solution)/shard_map/two_sections/pallas_call | solution.py:460
  21.3 1.4 %last_faces.1 = (f32[8,8,16,128]{3,2,1,0:T(8,128)}, f32[8]{0:T(128)}) custom-call(f32[8,12,32,128]{3,2,1,0:T(8,128)S(1)} %get-tuple-element.9.e0, f32[8,8,16,128]{3,2,1,0:T(8,128)S(1)} %get-tuple-element.10.acc, f32[8,9,16,128]{3,2,1,0:T(8,128)S(1)} %get-tuple-element.11.rf, f32[8,8,24,128]{3,2,1,0:T(8,128)S(1)} %get-tuple-element.12.fp, ...), custom_call_target="tpu_custom_call" | custom-call | tf_op jit(solution)/shard_map/last_faces/pallas_call | solution.py:480

commit v4 on v3

--- a/solution.py
+++ b/solution.py
@@ -22,7 +22,7 @@
 NW = 16
 NT = 128
 PAD = 8
-ROWS = 32
+ROWS = 40
 XN, ZC, YN = 4, 16, 4
 RADIAL = XN * ZC
 VMEM_LIMIT = 24 << 20
@@ -394,7 +394,7 @@
     gt[RD + 4 : 16, :] = jnp.zeros((4, NT), jnp.float32)
     enclosed = jnp.broadcast_to(jnp.sum(gt[...], axis=1, keepdims=True), (16, NT)) + core_ref[0]
     diagonal = lax.broadcasted_iota(jnp.int32, (16, NT), 1) + 2 == row
-    enc_v[...] = jnp.sum(jnp.where(diagonal, enclosed, 0.0), axis=0, keepdims=True)
+    enc_v[...] = jnp.sum(jnp.where(diagonal, enclosed, 0.0), axis=0)[:RD]
     gt[...] = enclosed * tb[3]
 
     def pull_down(k, rows):
@@ -434,7 +434,8 @@
 
 
 def last_kernel(e0, acc, rf, fp, tb, polar, enc_v, out_ref, enc_ref, out_v, sem):
-    enc_ref[...] = enc_v[0, :][:RD]
+    enc_store = pltpu.make_async_copy(enc_v, enc_ref, sem.at[RD])
+    enc_store.start()
 
     def put(v, k, h, value):
         out_v[v, k, 8 * h : 8 * h + 8, :] = 0.5 * (e0[v, k + 2, PAD + 8 * h : PAD + 8 * h + 8, :] + value)
@@ -445,6 +446,7 @@
     finish_zones(acc, rf, fp, tb, polar, put, lambda k: store(k).start())
     for k in range(RD):
         store(k).wait()
+    enc_store.wait()
 
 
 def body(conserved, core_mass):
@@ -460,7 +462,7 @@
     held = pl.pallas_call(
         kernel,
         out_shape=(
-            extended, slab, radial_flux, azimuth_fluxes, vmem((5, 16, NT), f32), vmem((8, NT), f32), vmem((1, NT), f32),
+            extended, slab, radial_flux, azimuth_fluxes, vmem((5, 16, NT), f32), vmem((8, NT), f32), vmem((RD,), f32),
         ),
         in_specs=[anywhere, pl.BlockSpec(memory_space=pltpu.SMEM), anywhere],
         out_specs=(resident,) * 7,
@@ -481,8 +483,8 @@
         last_kernel,
         out_shape=(jax.ShapeDtypeStruct(conserved.shape, f32), jax.ShapeDtypeStruct((RD,), f32)),
         in_specs=[resident] * 7,
-        out_specs=(anywhere, resident),
-        scratch_shapes=[slab, dma((RD,))],
+        out_specs=(anywhere, anywhere),
+        scratch_shapes=[slab, dma((RD + 1,))],
         compiler_params=pltpu.CompilerParams(vmem_limit_bytes=VMEM_LIMIT),
         name="last_faces",
     )(e0, acc, rf, fp, tb, polar, enc_v)

time: 23.1 us -> 22.4 us (0.970)
  Pallas kernels: 21.4 us -> 20.7 us
    pallas_call x1, Pallas kernels: 1.39 us -> 0.89 us  [body(): pl.pallas_call(last_kernel, out_shape=(jax.ShapeDtypeStruct(conserved.sha...]
    pallas_call x1, Pallas kernels: 20.1 us -> 19.8 us  [body(): pl.pallas_call(kernel, out_shape=(extended, slab, radial_flux, azimuth_fl...]
where the time goes in v4:
time: 22.4 us; the launch traced here: 22 us
  Pallas kernels  20.7 us (92%)
  between operations  1.28 us (6%)
    pallas_call x1, Pallas kernels, body(): pl.pallas_call(kernel, out_shape=(extended, slab, radial_flux, azimuth_fl...  19.8 us
    pallas_call x1, Pallas kernels, body(): pl.pallas_call(last_kernel, out_shape=(jax.ShapeDtypeStruct(conserved.sha...  0.89 us

profile of v4, /device:TPU:1, one launch (start us, length us, event | category | flops | bytes accessed | tf_op | source)
XLA Modules:
  0.0 22.0 jit_solution(8258649130997837461)
XLA Ops:
  1.3 19.8 %two_sections.1 = (f32[8,12,40,128]{3,2,1,0:T(8,128)S(1)}, f32[8,8,16,128]{3,2,1,0:T(8,128)S(1)}, f32[8,9,16,128]{3,2,1,0:T(8,128)S(1)}, f32[8,8,24,128]{3,2,1,0...) custom-call(f32[8,8,16,128]{3,2,1,0:T(8,128)} %x_ref.1, f32[1]{0:T(128)S(6)} %copy.5.core_ref, ...), custom_call_target="tpu_custom_call" | custom-call | tf_op jit(solution)/shard_map/two_sections/pallas_call | solution.py:462
  21.1 0.9 %last_faces.1 = (f32[8,8,16,128]{3,2,1,0:T(8,128)}, f32[8]{0:T(128)}) custom-call(f32[8,12,40,128]{3,2,1,0:T(8,128)S(1)} %get-tuple-element.9.e0, f32[8,8,16,128]{3,2,1,0:T(8,128)S(1)} %get-tuple-element.10.acc, f32[8,9,16,128]{3,2,1,0:T(8,128)S(1)} %get-tuple-element.11.rf, f32[8,8,24,128]{3,2,1,0:T(8,128)S(1)} %get-tuple-element.12.fp, ...), custom_call_target="tpu_custom_call" | custom-call | tf_op jit(solution)/shard_map/last_faces/pallas_call | solution.py:482
